TPU v7x, 32 devices: a whole 2x2x4 slice. The times are simulated.
32 devices in a mesh: group: 2 (over core), gx: 4 (over y, x), gy: 4 (over z).
Axes of the slice: x: 2, y: 2, z: 4, core: 2. Of those that a mesh axis runs over, the one named last changes fastest.
Arguments:
- forcing: float32 [2, 80, 32, 1024], P('group', None, 'gx', 'gy'), may hold values from -24 to 24
- conduct: bfloat16 [2, 80, 32, 1024], P('group', None, 'gx', 'gy'), may hold values from 0.25 to 4
- diag_add: bfloat16 [2, 80, 32, 1024], P('group', None, 'gx', 'gy'), may hold values from 0.049804688 to 0.5
- ice_mask: int32 [32, 1024], P('gx', 'gy'), may hold values 0 or 1
- grounded: int32 [32, 1024], P('gx', 'gy'), may hold values 0 or 1
Outputs:
- solution: float32 [2, 80, 32, 1024], P('group', None, 'gx', 'gy')
- residual: float32 [2, 80, 32, 1024], P('group', None, 'gx', 'gy')
All inputs are finite; a program needn't handle non-finite values. No bound on the sum of `ice_mask` or of `grounded` on one device may be relied on, other than what follows from the above.
Results may differ from a plain program's by a relative error of at most 0.0003.
Values sent between devices are 32-bit elements; how exact they have to be, the bound alone decides.
No kernel may reach another device: no remote copies, remote signals or barrier semaphores. Data moves between devices by JAX's collectives and lax.ppermute only.
A program may use at most 64 MiB of HBM per device.

v0:
```python
import jax
import jax.numpy as jnp
from jax import lax
from jax.sharding import PartitionSpec as P

ITERS = 6
far_weight = 0.25
cross_weight = 0.5
vertical_weight = 4.0
friction_gain = 8.0
NEIGHBOURS = (
    (1, 0, 1.0),
    (-1, 0, 1.0),
    (0, 1, 1.0),
    (0, -1, 1.0),
    (2, 0, far_weight),
    (-2, 0, far_weight),
    (0, 2, far_weight),
    (0, -2, far_weight),
    (1, 1, cross_weight),
    (1, -1, cross_weight),
    (-1, 1, cross_weight),
    (-1, -1, cross_weight),
)


def with_halo(block, sides, width):
    for axis, dim in sides:
        count = lax.axis_size(axis)
        forward = [(i, i + 1) for i in range(count - 1)]
        backward = [(target, source) for source, target in forward]
        low = lax.ppermute(
            lax.slice_in_dim(block, block.shape[dim] - width, None, axis=dim), axis, forward
        )
        high = lax.ppermute(lax.slice_in_dim(block, 0, width, axis=dim), axis, backward)
        block = jnp.concatenate([low, block, high], axis=dim)
    return block


def from_partner(shard, axis, distance):
    return lax.ppermute(shard, axis, [(i, i ^ 1 << distance) for i in range(lax.axis_size(axis))])


def beside_sum(padded, extent_x, extent_y):
    summed = jnp.zeros((padded.shape[0], extent_x, extent_y), jnp.float32)
    for shift_x, shift_y, weight in NEIGHBOURS:
        summed = (
            summed
            + weight
            * padded[:, 2 + shift_x : 2 + shift_x + extent_x, 2 + shift_y : 2 + shift_y + extent_y]
        )
    return summed


def vertical_sum(values):
    zeroes = jnp.zeros_like(values[:1])
    return jnp.concatenate([values[1:], zeroes], 0) + jnp.concatenate([zeroes, values[:-1]], 0)


def spread_padded(padded, values):
    return beside_sum(padded, values.shape[1], values.shape[2]) + vertical_weight * vertical_sum(
        values
    )


def operate(vector, coupling, diagonal):
    scaled = coupling * vector
    padded = with_halo(scaled, (("gx", 1), ("gy", 2)), 2)
    return diagonal * vector - coupling * spread_padded(padded, scaled)


def paired_sums(residual, precond, applied):
    return lax.psum((jnp.sum(residual * precond), jnp.sum(applied * precond)), ("gx", "gy"))


def on_device(forcing, conduct, diag_add, ice_mask, grounded):
    own_force = forcing[0]
    layers = own_force.shape[0]
    group_id = lax.axis_index("group")
    is_ice = (group_id == 0).astype(jnp.float32)
    ice_cells = ice_mask.astype(jnp.float32)
    ground_cells = grounded.astype(jnp.float32)
    active = ice_cells * (1.0 - (1.0 - is_ice) * ground_cells)
    coupling = jnp.sqrt(conduct[0].astype(jnp.float32)) * active
    layer_index = lax.broadcasted_iota(jnp.int32, (layers, 1, 1), 0)
    edge_layer = jnp.where(group_id == 0, 0, layers - 1).astype(jnp.int32)
    edge_pick = (layer_index == edge_layer).astype(jnp.float32)
    bottom = (layer_index == 0).astype(jnp.float32)
    base_diag = diag_add[0].astype(jnp.float32) + bottom * (
        is_ice * friction_gain * ground_cells * ice_cells
    )
    padded_coupling = with_halo(coupling, (("gx", 1), ("gy", 2)), 2)
    diagonal = base_diag + coupling * spread_padded(padded_coupling, coupling)
    shared_value = active * jnp.mean(own_force, axis=0)
    shared_weight = lax.dynamic_index_in_dim(coupling, edge_layer, 0, keepdims=False)
    received = from_partner(jnp.stack([shared_value, shared_weight]), "group", 0)
    source = active * own_force + edge_pick * (active * received[1] * received[0])
    inverse = 1.0 / diagonal
    solution = jnp.zeros_like(source)
    residual = source
    precond = inverse * residual
    applied = operate(precond, coupling, diagonal)
    norm_now, curve = paired_sums(residual, precond, applied)
    step_size = norm_now / curve
    direction = precond
    along = applied
    for iteration in range(ITERS):
        solution = solution + step_size * direction
        residual = residual - step_size * along
        if iteration + 1 < ITERS:
            precond = inverse * residual
            applied = operate(precond, coupling, diagonal)
            norm_next, curve = paired_sums(residual, precond, applied)
            step_ratio = norm_next / norm_now
            step_size = norm_next / (curve - step_ratio * norm_next / step_size)
            direction = precond + step_ratio * direction
            along = applied + step_ratio * along
            norm_now = norm_next
    return (solution[None], residual[None])


def solution(mesh):
    in_specs = (
        P("group", None, "gx", "gy"),
        P("group", None, "gx", "gy"),
        P("group", None, "gx", "gy"),
        P("gx", "gy"),
        P("gx", "gy"),
    )
    out_specs = (P("group", None, "gx", "gy"), P("group", None, "gx", "gy"))
    return jax.shard_map(
        on_device, mesh=mesh, in_specs=in_specs, out_specs=out_specs, check_vma=False
    )
```

profile of v0, /device:TPU:0, one launch (start us, length us, event | category | flops | bytes accessed | tf_op | source)
XLA Modules:
  0.0 470.8 jit_solution(15038261008825120504)
XLA Ops:
  3.8 1.3 collective-permute-start.1
  5.1 5.5 %collective-permute-start.2 = (f32[80,2,256]{2,1,0:T(2,128)S(1)}, f32[80,2,256]{2,1,0:T(2,128)S(1)}, u32[]{:S(2)}, u32[]{:S(2)}) collective-permute-start(f32[80,2,256]{2,1,0:T(2,128)S(1)} %get-tuple-element.103), channel_id=1, source_target_pairs={{0,4},{4,8},{8,12},{1,5},{5,9},{9,13},{2,6},{6,10},{10,14},{3,7},{... | collective-permute-start | bytes 491528 | tf_op jit(solution)/shard_map/ppermute | solution.py:32
  16.4 4.5 collective-permute-start.4
  22.7 1.5 pad_maximum_fusion
  24.3 2.8 fusion.132
  27.3 1.3 collective-permute-start.5
  28.6 5.2 %collective-permute-start.6 = (f32[80,2,256]{2,1,0:T(2,128)S(1)}, f32[80,2,256]{2,1,0:T(2,128)S(1)}, u32[]{:S(2)}, u32[]{:S(2)}) collective-permute-start(f32[80,2,256]{2,1,0:T(2,128)S(1)} %get-tuple-element.99), channel_id=1, source_target_pairs={{0,4},{4,8},{8,12},{1,5},{5,9},{9,13},{2,6},{6,10},{10,14},{3,7},{... | collective-permute-start | bytes 491528 | tf_op jit(solution)/shard_map/ppermute | solution.py:32
  33.8 1.3 collective-permute-done.5
  35.1 1.5 collective-permute-done.6
  37.9 1.3 copy.18
  40.7 4.8 %collective-permute-start.8 = (f32[80,12,2]{0,2,1:T(2,128)S(1)}, f32[80,12,2]{0,2,1:T(2,128)S(1)}, u32[]{:S(2)}, u32[]{:S(2)}) collective-permute-start(f32[80,12,2]{0,2,1:T(2,128)S(1)} %copy.20), channel_id=1, source_target_pairs={{0,1},{1,2},{2,3},{4,5},{5,6},{6,7},{8,9},{9,10},{10,11},{12,13},{... | collective-permute-start | bytes 23048 | tf_op jit(solution)/shard_map/ppermute | solution.py:32
  49.0 2.9 pad_maximum_fusion.1
  52.0 3.4 multiply_reduce_fusion.10
  55.4 46.6 %all-reduce.19 = (f32[]{:T(128)}, f32[]{:T(128)}) all-reduce(f32[]{:T(128)} %get-tuple-element.15, f32[]{:T(128)} %get-tuple-element.14), channel_id=1, replica_groups=mesh['group'=2,'gx'=4,'gy'=4] {'gx','gy'}, use_global_device_ids=true, to_apply=%region_2.3 | all-reduce | flops 2 | bytes 16 | tf_op jit(solution)/shard_map/psum | solution.py:73
  103.4 1.5 fusion.131
  105.0 1.3 collective-permute-start.10
  106.3 1.3 collective-permute-start.9
  107.6 1.5 collective-permute-done.10
  109.1 4.4 collective-permute-done.9
  114.8 1.3 copy.22
  117.7 4.7 %collective-permute-start.12 = (f32[80,12,2]{0,2,1:T(2,128)S(1)}, f32[80,12,2]{0,2,1:T(2,128)S(1)}, u32[]{:S(2)}, u32[]{:S(2)}) collective-permute-start(f32[80,12,2]{0,2,1:T(2,128)S(1)} %copy.24), channel_id=1, source_target_pairs={{0,1},{1,2},{2,3},{4,5},{5,6},{6,7},{8,9},{9,10},{10,11},{12,13},{... | collective-permute-start | bytes 23048 | tf_op jit(solution)/shard_map/ppermute | solution.py:32
  125.1 2.7 pad_maximum_fusion.2
  127.8 3.5 multiply_reduce_fusion.8
  131.3 39.4 %all-reduce.18 = (f32[]{:T(128)}, f32[]{:T(128)}) all-reduce(f32[]{:T(128)} %get-tuple-element.11, f32[]{:T(128)} %get-tuple-element.10), channel_id=1, replica_groups=mesh['group'=2,'gx'=4,'gy'=4] {'gx','gy'}, use_global_device_ids=true, to_apply=%region_6.7 | all-reduce | flops 2 | bytes 16 | tf_op jit(solution)/shard_map/psum | solution.py:73
  175.4 1.6 fusion.130
  177.1 1.3 collective-permute-start.13
  178.4 4.6 collective-permute-start.14
  183.0 1.3 collective-permute-done.13
  184.3 1.5 collective-permute-done.14
  187.3 1.3 copy.26
  189.9 1.3 copy.28
  191.3 4.5 collective-permute-start.16
  199.3 2.9 pad_maximum_fusion.3
  202.2 3.4 multiply_reduce_fusion.6
  205.6 39.3 %all-reduce.17 = (f32[]{:T(128)}, f32[]{:T(128)}) all-reduce(f32[]{:T(128)} %get-tuple-element.9, f32[]{:T(128)} %get-tuple-element.8), channel_id=1, replica_groups=mesh['group'=2,'gx'=4,'gy'=4] {'gx','gy'}, use_global_device_ids=true, to_apply=%region_10.11 | all-reduce | flops 2 | bytes 16 | tf_op jit(solution)/shard_map/psum | solution.py:73
  248.7 2.7 fusion.129
  251.5 1.3 collective-permute-start.17
  252.8 4.6 collective-permute-start.18
  257.4 1.3 collective-permute-done.17
  258.8 1.5 collective-permute-done.18
  262.5 4.8 %collective-permute-start.20 = (f32[80,12,2]{0,2,1:T(2,128)S(1)}, f32[80,12,2]{0,2,1:T(2,128)S(1)}, u32[]{:S(2)}, u32[]{:S(2)}) collective-permute-start(f32[80,12,2]{0,2,1:T(2,128)S(1)} %copy.32), channel_id=1, source_target_pairs={{0,1},{1,2},{2,3},{4,5},{5,6},{6,7},{8,9},{9,10},{10,11},{12,13},{... | collective-permute-start | bytes 23048 | tf_op jit(solution)/shard_map/ppermute | solution.py:32
  269.2 1.5 pad_maximum_fusion.4
  270.7 3.5 multiply_reduce_fusion.4
  274.1 42.2 %all-reduce.16 = (f32[]{:T(128)}, f32[]{:T(128)}) all-reduce(f32[]{:T(128)} %get-tuple-element.7, f32[]{:T(128)} %get-tuple-element.6), channel_id=1, replica_groups=mesh['group'=2,'gx'=4,'gy'=4] {'gx','gy'}, use_global_device_ids=true, to_apply=%region_14.15 | all-reduce | flops 2 | bytes 16 | tf_op jit(solution)/shard_map/psum | solution.py:73
  320.1 1.8 fusion.128
  323.3 4.6 collective-permute-start.22
  327.9 1.3 collective-permute-done.21
  329.2 1.5 collective-permute-done.22
  332.0 1.3 copy.34
  334.8 4.5 collective-permute-start.24
  342.1 2.7 pad_maximum_fusion.5
  344.8 3.4 multiply_reduce_fusion.2
  348.2 40.5 %all-reduce.15 = (f32[]{:T(128)}, f32[]{:T(128)}) all-reduce(f32[]{:T(128)} %get-tuple-element.5, f32[]{:T(128)} %get-tuple-element.4), channel_id=1, replica_groups=mesh['group'=2,'gx'=4,'gy'=4] {'gx','gy'}, use_global_device_ids=true, to_apply=%region_18.19 | all-reduce | flops 2 | bytes 16 | tf_op jit(solution)/shard_map/psum | solution.py:73
  392.7 2.7 fusion.127
  395.5 1.3 collective-permute-start.25
  396.8 4.6 collective-permute-start.26
  401.4 1.4 collective-permute-done.25
  402.8 1.4 collective-permute-done.26
  405.5 1.3 copy.38
  408.4 4.8 %collective-permute-start.28 = (f32[80,12,2]{0,2,1:T(2,128)S(1)}, f32[80,12,2]{0,2,1:T(2,128)S(1)}, u32[]{:S(2)}, u32[]{:S(2)}) collective-permute-start(f32[80,12,2]{0,2,1:T(2,128)S(1)} %copy.40), channel_id=1, source_target_pairs={{0,1},{1,2},{2,3},{4,5},{5,6},{6,7},{8,9},{9,10},{10,11},{12,13},{... | collective-permute-start | bytes 23048 | tf_op jit(solution)/shard_map/ppermute | solution.py:32
  415.8 2.7 pad_maximum_fusion.6
  418.6 3.4 multiply_reduce_fusion
  422.0 40.5 %all-reduce.14 = (f32[]{:T(128)}, f32[]{:T(128)}) all-reduce(f32[]{:T(128)} %get-tuple-element.13, f32[]{:T(128)} %get-tuple-element.12), channel_id=1, replica_groups=mesh['group'=2,'gx'=4,'gy'=4] {'gx','gy'}, use_global_device_ids=true, to_apply=%region_22.23 | all-reduce | flops 2 | bytes 16 | tf_op jit(solution)/shard_map/psum | solution.py:73
  466.7 3.2 add_bitcast_fusion
  (140 shorter events, 46.9 us)
Async XLA Ops:
  3.8 9.1 %collective-permute-start.1 = (f32[80,2,256]{2,1,0:T(2,128)S(1)}, f32[80,2,256]{2,1,0:T(2,128)S(1)}, u32[]{:S(2)}, u32[]{:S(2)}) collective-permute-start(f32[80,2,256]{2,1,0:T(2,128)S(1)} %get-tuple-element.104), channel_id=1, source_target_pairs={{4,0},{8,4},{12,8},{5,1},{9,5},{13,9},{6,2},{10,6},{14,10},{7,3},{... | collective-permute-start | bytes 491528 | tf_op jit(solution)/shard_map/ppermute | solution.py:35
  5.1 8.9 %collective-permute-start.2 = (f32[80,2,256]{2,1,0:T(2,128)S(1)}, f32[80,2,256]{2,1,0:T(2,128)S(1)}, u32[]{:S(2)}, u32[]{:S(2)}) collective-permute-start(f32[80,2,256]{2,1,0:T(2,128)S(1)} %get-tuple-element.103), channel_id=1, source_target_pairs={{0,4},{4,8},{8,12},{1,5},{5,9},{9,13},{2,6},{6,10},{10,14},{3,7},{... | collective-permute-start | bytes 491528 | tf_op jit(solution)/shard_map/ppermute | solution.py:32
  10.7 10.3 %collective-permute-start = (f32[2,8,256]{2,1,0:T(8,128)S(1)}, f32[2,8,256]{2,1,0:T(8,128)S(1)}, u32[]{:S(2)}, u32[]{:S(2)}) collective-permute-start(f32[2,8,256]{2,1,0:T(8,128)S(1)} %pad_maximum_fusion.28), channel_id=1, source_target_pairs={{0,16},{16,0},{1,17},{17,1},{2,18},{18,2},{3,19},{19,3},{4,20},{20... | collective-permute-start | bytes 49160 | tf_op jit(solution)/shard_map/ppermute | solution.py:41
  14.8 6.1 %collective-permute-start.3 = (f32[80,12,2]{0,2,1:T(2,128)S(1)}, f32[80,12,2]{0,2,1:T(2,128)S(1)}, u32[]{:S(2)}, u32[]{:S(2)}) collective-permute-start(f32[80,12,2]{0,2,1:T(2,128)S(1)} %copy.14), channel_id=1, source_target_pairs={{1,0},{2,1},{3,2},{5,4},{6,5},{7,6},{9,8},{10,9},{11,10},{13,12},{... | collective-permute-start | bytes 23048 | tf_op jit(solution)/shard_map/ppermute | solution.py:35
  16.4 5.9 %collective-permute-start.4 = (f32[80,12,2]{0,2,1:T(2,128)S(1)}, f32[80,12,2]{0,2,1:T(2,128)S(1)}, u32[]{:S(2)}, u32[]{:S(2)}) collective-permute-start(f32[80,12,2]{0,2,1:T(2,128)S(1)} %copy.16), channel_id=1, source_target_pairs={{0,1},{1,2},{2,3},{4,5},{5,6},{6,7},{8,9},{9,10},{10,11},{12,13},{... | collective-permute-start | bytes 23048 | tf_op jit(solution)/shard_map/ppermute | solution.py:32
  22.7 1.5 copy-start
  22.7 1.5 copy-start.1
  22.7 1.5 copy-start.13
  22.7 1.6 copy-start.14
  22.7 1.6 copy-start.27
  27.3 7.8 %collective-permute-start.5 = (f32[80,2,256]{2,1,0:T(2,128)S(1)}, f32[80,2,256]{2,1,0:T(2,128)S(1)}, u32[]{:S(2)}, u32[]{:S(2)}) collective-permute-start(f32[80,2,256]{2,1,0:T(2,128)S(1)} %get-tuple-element.100), channel_id=1, source_target_pairs={{4,0},{8,4},{12,8},{5,1},{9,5},{13,9},{6,2},{10,6},{14,10},{7,3},{... | collective-permute-start | bytes 491528 | tf_op jit(solution)/shard_map/ppermute | solution.py:35
  28.6 8.0 %collective-permute-start.6 = (f32[80,2,256]{2,1,0:T(2,128)S(1)}, f32[80,2,256]{2,1,0:T(2,128)S(1)}, u32[]{:S(2)}, u32[]{:S(2)}) collective-permute-start(f32[80,2,256]{2,1,0:T(2,128)S(1)} %get-tuple-element.99), channel_id=1, source_target_pairs={{0,4},{4,8},{8,12},{1,5},{5,9},{9,13},{2,6},{6,10},{10,14},{3,7},{... | collective-permute-start | bytes 491528 | tf_op jit(solution)/shard_map/ppermute | solution.py:32
  39.2 7.5 %collective-permute-start.7 = (f32[80,12,2]{0,2,1:T(2,128)S(1)}, f32[80,12,2]{0,2,1:T(2,128)S(1)}, u32[]{:S(2)}, u32[]{:S(2)}) collective-permute-start(f32[80,12,2]{0,2,1:T(2,128)S(1)} %copy.18), channel_id=1, source_target_pairs={{1,0},{2,1},{3,2},{5,4},{6,5},{7,6},{9,8},{10,9},{11,10},{13,12},{... | collective-permute-start | bytes 23048 | tf_op jit(solution)/shard_map/ppermute | solution.py:35
  40.7 7.1 %collective-permute-start.8 = (f32[80,12,2]{0,2,1:T(2,128)S(1)}, f32[80,12,2]{0,2,1:T(2,128)S(1)}, u32[]{:S(2)}, u32[]{:S(2)}) collective-permute-start(f32[80,12,2]{0,2,1:T(2,128)S(1)} %copy.20), channel_id=1, source_target_pairs={{0,1},{1,2},{2,3},{4,5},{5,6},{6,7},{8,9},{9,10},{10,11},{12,13},{... | collective-permute-start | bytes 23048 | tf_op jit(solution)/shard_map/ppermute | solution.py:32
  49.0 2.9 copy-start.7
  49.0 2.9 copy-start.17
  49.0 2.9 copy-start.18
  104.9 22.9 %copy-start.6 = (f32[80,8,256]{2,1,0:T(8,128)}, f32[80,8,256]{2,1,0:T(8,128)S(1)}, u32[]{:S(2)}) copy-start(f32[80,8,256]{2,1,0:T(8,128)S(1)} %get-tuple-element.44) | copy-start | bytes 1966084
  105.0 4.1 collective-permute-start.10
  106.3 7.2 %collective-permute-start.9 = (f32[80,2,256]{2,1,0:T(2,128)S(1)}, f32[80,2,256]{2,1,0:T(2,128)S(1)}, u32[]{:S(2)}, u32[]{:S(2)}) collective-permute-start(f32[80,2,256]{2,1,0:T(2,128)S(1)} %get-tuple-element.96), channel_id=1, source_target_pairs={{4,0},{8,4},{12,8},{5,1},{9,5},{13,9},{6,2},{10,6},{14,10},{7,3},{... | collective-permute-start | bytes 491528 | tf_op jit(solution)/shard_map/ppermute | solution.py:35
  116.2 7.4 %collective-permute-start.11 = (f32[80,12,2]{0,2,1:T(2,128)S(1)}, f32[80,12,2]{0,2,1:T(2,128)S(1)}, u32[]{:S(2)}, u32[]{:S(2)}) collective-permute-start(f32[80,12,2]{0,2,1:T(2,128)S(1)} %copy.22), channel_id=1, source_target_pairs={{1,0},{2,1},{3,2},{5,4},{6,5},{7,6},{9,8},{10,9},{11,10},{13,12},{... | collective-permute-start | bytes 23048 | tf_op jit(solution)/shard_map/ppermute | solution.py:35
  117.7 6.2 %collective-permute-start.12 = (f32[80,12,2]{0,2,1:T(2,128)S(1)}, f32[80,12,2]{0,2,1:T(2,128)S(1)}, u32[]{:S(2)}, u32[]{:S(2)}) collective-permute-start(f32[80,12,2]{0,2,1:T(2,128)S(1)} %copy.24), channel_id=1, source_target_pairs={{0,1},{1,2},{2,3},{4,5},{5,6},{6,7},{8,9},{9,10},{10,11},{12,13},{... | collective-permute-start | bytes 23048 | tf_op jit(solution)/shard_map/ppermute | solution.py:32
  125.1 2.7 copy-start.19
  125.1 2.7 copy-start.20
  127.8 47.6 %copy-start.2 = (f32[80,8,256]{2,1,0:T(8,128)S(1)}, f32[80,8,256]{2,1,0:T(8,128)}, u32[]{:S(2)}) copy-start(f32[80,8,256]{2,1,0:T(8,128)} %get-tuple-element.45) | copy-start | bytes 1966084
  177.0 71.7 %copy-start.3 = (f32[80,8,256]{2,1,0:T(8,128)}, f32[80,8,256]{2,1,0:T(8,128)S(1)}, u32[]{:S(2)}) copy-start(f32[80,8,256]{2,1,0:T(8,128)S(1)} %get-tuple-element.41) | copy-start | bytes 1966084
  177.1 7.2 %collective-permute-start.13 = (f32[80,2,256]{2,1,0:T(2,128)S(1)}, f32[80,2,256]{2,1,0:T(2,128)S(1)}, u32[]{:S(2)}, u32[]{:S(2)}) collective-permute-start(f32[80,2,256]{2,1,0:T(2,128)S(1)} %get-tuple-element.92), channel_id=1, source_target_pairs={{4,0},{8,4},{12,8},{5,1},{9,5},{13,9},{6,2},{10,6},{14,10},{7,3},{... | collective-permute-start | bytes 491528 | tf_op jit(solution)/shard_map/ppermute | solution.py:35
  178.4 7.4 %collective-permute-start.14 = (f32[80,2,256]{2,1,0:T(2,128)S(1)}, f32[80,2,256]{2,1,0:T(2,128)S(1)}, u32[]{:S(2)}, u32[]{:S(2)}) collective-permute-start(f32[80,2,256]{2,1,0:T(2,128)S(1)} %get-tuple-element.91), channel_id=1, source_target_pairs={{0,4},{4,8},{8,12},{1,5},{5,9},{9,13},{2,6},{6,10},{10,14},{3,7},{... | collective-permute-start | bytes 491528 | tf_op jit(solution)/shard_map/ppermute | solution.py:32
  188.7 8.3 %collective-permute-start.15 = (f32[80,12,2]{0,2,1:T(2,128)S(1)}, f32[80,12,2]{0,2,1:T(2,128)S(1)}, u32[]{:S(2)}, u32[]{:S(2)}) collective-permute-start(f32[80,12,2]{0,2,1:T(2,128)S(1)} %copy.26), channel_id=1, source_target_pairs={{1,0},{2,1},{3,2},{5,4},{6,5},{7,6},{9,8},{10,9},{11,10},{13,12},{... | collective-permute-start | bytes 23048 | tf_op jit(solution)/shard_map/ppermute | solution.py:35
  191.3 6.8 %collective-permute-start.16 = (f32[80,12,2]{0,2,1:T(2,128)S(1)}, f32[80,12,2]{0,2,1:T(2,128)S(1)}, u32[]{:S(2)}, u32[]{:S(2)}) collective-permute-start(f32[80,12,2]{0,2,1:T(2,128)S(1)} %copy.28), channel_id=1, source_target_pairs={{0,1},{1,2},{2,3},{4,5},{5,6},{6,7},{8,9},{9,10},{10,11},{12,13},{... | collective-permute-start | bytes 23048 | tf_op jit(solution)/shard_map/ppermute | solution.py:32
  199.3 2.9 copy-start.21
  199.3 2.9 copy-start.22
  251.5 7.2 %collective-permute-start.17 = (f32[80,2,256]{2,1,0:T(2,128)S(1)}, f32[80,2,256]{2,1,0:T(2,128)S(1)}, u32[]{:S(2)}, u32[]{:S(2)}) collective-permute-start(f32[80,2,256]{2,1,0:T(2,128)S(1)} %get-tuple-element.88), channel_id=1, source_target_pairs={{4,0},{8,4},{12,8},{5,1},{9,5},{13,9},{6,2},{10,6},{14,10},{7,3},{... | collective-permute-start | bytes 491528 | tf_op jit(solution)/shard_map/ppermute | solution.py:35
  252.8 7.4 %collective-permute-start.18 = (f32[80,2,256]{2,1,0:T(2,128)S(1)}, f32[80,2,256]{2,1,0:T(2,128)S(1)}, u32[]{:S(2)}, u32[]{:S(2)}) collective-permute-start(f32[80,2,256]{2,1,0:T(2,128)S(1)} %get-tuple-element.87), channel_id=1, source_target_pairs={{0,4},{4,8},{8,12},{1,5},{5,9},{9,13},{2,6},{6,10},{10,14},{3,7},{... | collective-permute-start | bytes 491528 | tf_op jit(solution)/shard_map/ppermute | solution.py:32
  261.0 7.5 %collective-permute-start.19 = (f32[80,12,2]{0,2,1:T(2,128)S(1)}, f32[80,12,2]{0,2,1:T(2,128)S(1)}, u32[]{:S(2)}, u32[]{:S(2)}) collective-permute-start(f32[80,12,2]{0,2,1:T(2,128)S(1)} %copy.30), channel_id=1, source_target_pairs={{1,0},{2,1},{3,2},{5,4},{6,5},{7,6},{9,8},{10,9},{11,10},{13,12},{... | collective-permute-start | bytes 23048 | tf_op jit(solution)/shard_map/ppermute | solution.py:35
  262.5 6.3 %collective-permute-start.20 = (f32[80,12,2]{0,2,1:T(2,128)S(1)}, f32[80,12,2]{0,2,1:T(2,128)S(1)}, u32[]{:S(2)}, u32[]{:S(2)}) collective-permute-start(f32[80,12,2]{0,2,1:T(2,128)S(1)} %copy.32), channel_id=1, source_target_pairs={{0,1},{1,2},{2,3},{4,5},{5,6},{6,7},{8,9},{9,10},{10,11},{12,13},{... | collective-permute-start | bytes 23048 | tf_op jit(solution)/shard_map/ppermute | solution.py:32
  269.2 1.5 copy-start.5
  269.2 1.5 copy-start.25
  269.2 1.5 copy-start.26
  322.0 7.2 %collective-permute-start.21 = (f32[80,2,256]{2,1,0:T(2,128)S(1)}, f32[80,2,256]{2,1,0:T(2,128)S(1)}, u32[]{:S(2)}, u32[]{:S(2)}) collective-permute-start(f32[80,2,256]{2,1,0:T(2,128)S(1)} %get-tuple-element.84), channel_id=1, source_target_pairs={{4,0},{8,4},{12,8},{5,1},{9,5},{13,9},{6,2},{10,6},{14,10},{7,3},{... | collective-permute-start | bytes 491528 | tf_op jit(solution)/shard_map/ppermute | solution.py:35
  323.3 7.4 %collective-permute-start.22 = (f32[80,2,256]{2,1,0:T(2,128)S(1)}, f32[80,2,256]{2,1,0:T(2,128)S(1)}, u32[]{:S(2)}, u32[]{:S(2)}) collective-permute-start(f32[80,2,256]{2,1,0:T(2,128)S(1)} %get-tuple-element.83), channel_id=1, source_target_pairs={{0,4},{4,8},{8,12},{1,5},{5,9},{9,13},{2,6},{6,10},{10,14},{3,7},{... | collective-permute-start | bytes 491528 | tf_op jit(solution)/shard_map/ppermute | solution.py:32
  333.3 7.2 %collective-permute-start.23 = (f32[80,12,2]{0,2,1:T(2,128)S(1)}, f32[80,12,2]{0,2,1:T(2,128)S(1)}, u32[]{:S(2)}, u32[]{:S(2)}) collective-permute-start(f32[80,12,2]{0,2,1:T(2,128)S(1)} %copy.34), channel_id=1, source_target_pairs={{1,0},{2,1},{3,2},{5,4},{6,5},{7,6},{9,8},{10,9},{11,10},{13,12},{... | collective-permute-start | bytes 23048 | tf_op jit(solution)/shard_map/ppermute | solution.py:35
  334.8 6.0 %collective-permute-start.24 = (f32[80,12,2]{0,2,1:T(2,128)S(1)}, f32[80,12,2]{0,2,1:T(2,128)S(1)}, u32[]{:S(2)}, u32[]{:S(2)}) collective-permute-start(f32[80,12,2]{0,2,1:T(2,128)S(1)} %copy.36), channel_id=1, source_target_pairs={{0,1},{1,2},{2,3},{4,5},{5,6},{6,7},{8,9},{9,10},{10,11},{12,13},{... | collective-permute-start | bytes 23048 | tf_op jit(solution)/shard_map/ppermute | solution.py:32
  342.1 2.7 copy-start.23
  342.1 2.7 copy-start.24
  344.8 47.9 %copy-start.8 = (f32[80,8,256]{2,1,0:T(8,128)S(1)}, f32[80,8,256]{2,1,0:T(8,128)}, u32[]{:S(2)}) copy-start(f32[80,8,256]{2,1,0:T(8,128)} %get-tuple-element.35) | copy-start | bytes 1966084
  395.5 7.3 %collective-permute-start.25 = (f32[80,2,256]{2,1,0:T(2,128)S(1)}, f32[80,2,256]{2,1,0:T(2,128)S(1)}, u32[]{:S(2)}, u32[]{:S(2)}) collective-permute-start(f32[80,2,256]{2,1,0:T(2,128)S(1)} %get-tuple-element.80), channel_id=1, source_target_pairs={{4,0},{8,4},{12,8},{5,1},{9,5},{13,9},{6,2},{10,6},{14,10},{7,3},{... | collective-permute-start | bytes 491528 | tf_op jit(solution)/shard_map/ppermute | solution.py:35
  396.8 7.4 %collective-permute-start.26 = (f32[80,2,256]{2,1,0:T(2,128)S(1)}, f32[80,2,256]{2,1,0:T(2,128)S(1)}, u32[]{:S(2)}, u32[]{:S(2)}) collective-permute-start(f32[80,2,256]{2,1,0:T(2,128)S(1)} %get-tuple-element.79), channel_id=1, source_target_pairs={{0,4},{4,8},{8,12},{1,5},{5,9},{9,13},{2,6},{6,10},{10,14},{3,7},{... | collective-permute-start | bytes 491528 | tf_op jit(solution)/shard_map/ppermute | solution.py:32
  406.8 7.5 %collective-permute-start.27 = (f32[80,12,2]{0,2,1:T(2,128)S(1)}, f32[80,12,2]{0,2,1:T(2,128)S(1)}, u32[]{:S(2)}, u32[]{:S(2)}) collective-permute-start(f32[80,12,2]{0,2,1:T(2,128)S(1)} %copy.38), channel_id=1, source_target_pairs={{1,0},{2,1},{3,2},{5,4},{6,5},{7,6},{9,8},{10,9},{11,10},{13,12},{... | collective-permute-start | bytes 23048 | tf_op jit(solution)/shard_map/ppermute | solution.py:35
  408.4 6.3 %collective-permute-start.28 = (f32[80,12,2]{0,2,1:T(2,128)S(1)}, f32[80,12,2]{0,2,1:T(2,128)S(1)}, u32[]{:S(2)}, u32[]{:S(2)}) collective-permute-start(f32[80,12,2]{0,2,1:T(2,128)S(1)} %copy.40), channel_id=1, source_target_pairs={{0,1},{1,2},{2,3},{4,5},{5,6},{6,7},{8,9},{9,10},{10,11},{12,13},{... | collective-permute-start | bytes 23048 | tf_op jit(solution)/shard_map/ppermute | solution.py:32
  415.8 2.7 copy-start.9
  415.8 2.7 copy-start.11
  415.8 2.7 copy-start.15
  415.8 2.8 copy-start.16
  418.6 48.0 %copy-start.4 = (f32[80,8,256]{2,1,0:T(8,128)S(1)}, f32[80,8,256]{2,1,0:T(8,128)}, u32[]{:S(2)}) copy-start(f32[80,8,256]{2,1,0:T(8,128)} %copy-done.3) | copy-start | bytes 1966084
  466.7 3.2 copy-start.10
  466.7 3.2 copy-start.12
where the time goes:
time: 473 us; the launch traced here: 471 us
  blocking collectives  249 us (53%)
  starting transfers between devices  81 us (17%)
  other arithmetic  59.5 us (13%)
  local copies, waits for them, and re-layouts  35.4 us (7%)
  waiting for transfers between devices  23.2 us (5%)
  between operations  23.2 us (5%)
    psum x6, blocking collectives, paired_sums(): lax.psum((jnp.sum(residual * precond), jnp.sum(applied * precond)), ('gx'...  249 us
    ppermute x14, starting transfers between devices, with_halo(): lax.ppermute(lax.slice_in_dim(block, block.shape[dim] - width, None, axis...  62.9 us
    reduce_sum x6, other arithmetic, paired_sums(): jnp.sum(applied * precond)  20.6 us
    concatenate x14, other arithmetic, with_halo(): block = jnp.concatenate([low, block, high], axis=dim)  18.5 us
    ppermute x14, starting transfers between devices, with_halo(): lax.ppermute(lax.slice_in_dim(block, 0, width, axis=dim), axis, backward)  18 us
    mul x6, other arithmetic, operate(): scaled = coupling * vector  13.2 us
    slice x14, local copies, waits for them, and re-layouts, with_halo(): lax.slice_in_dim(block, 0, width, axis=dim)  13.1 us
    ppermute x14, waiting for transfers between devices, with_halo(): lax.ppermute(lax.slice_in_dim(block, 0, width, axis=dim), axis, backward)  12.2 us
  transfers between devices with their start and end apart: 29, of which 15 were waited for; matrix products, arithmetic and copies ran while one was open for 3% of the time, Pallas kernels for 0%

commit v1 on v0

--- a/solution.py
+++ b/solution.py
@@ -70,7 +70,13 @@
 
 
 def paired_sums(residual, precond, applied):
-    return lax.psum((jnp.sum(residual * precond), jnp.sum(applied * precond)), ("gx", "gy"))
+
+    def _bind_body(point):
+        reply = jax.lax.psum(point, "gy")
+        side_arr = jax.lax.psum(reply, "gx")
+        return side_arr
+
+    return _bind_body((jnp.sum(residual * precond), jnp.sum(applied * precond)))
 
 
 def on_device(forcing, conduct, diag_add, ice_mask, grounded):

time: 473 us -> 361 us (0.76)
  blocking collectives: 249 us -> 137 us
    psum x6 -> x12, blocking collectives: 249 us -> 137 us  [the longest x6 69.4 us: _bind_body(): side_arr = jax.lax.psum(reply, 'gx')]
  transfers between devices with their start and end apart: 29 -> 29, of which waited for: 15 -> 15; matrix products, arithmetic and copies ran while one was open for 3% -> 4% of each run, Pallas kernels for 0% -> 0%
where the time goes in v1:
time: 361 us; the launch traced here: 359 us
  blocking collectives  137 us (38%)
  starting transfers between devices  81.6 us (23%)
  other arithmetic  59.4 us (16%)
  local copies, waits for them, and re-layouts  35.4 us (10%)
  waiting for transfers between devices  23.2 us (6%)
  between operations  22.6 us (6%)
    psum x6, blocking collectives, _bind_body(): side_arr = jax.lax.psum(reply, 'gx')  69.4 us
    psum x6, blocking collectives, _bind_body(): reply = jax.lax.psum(point, 'gy')  67.4 us
    ppermute x14, starting transfers between devices, with_halo(): lax.ppermute(lax.slice_in_dim(block, block.shape[dim] - width, None, axis...  63.5 us
    reduce_sum x6, other arithmetic, paired_sums(): return _bind_body((jnp.sum(residual * precond), jnp.sum(applied * precond)))  20.4 us
    concatenate x14, other arithmetic, with_halo(): block = jnp.concatenate([low, block, high], axis=dim)  18.5 us
    ppermute x14, starting transfers between devices, with_halo(): lax.ppermute(lax.slice_in_dim(block, 0, width, axis=dim), axis, backward)  18 us
    mul x6, other arithmetic, operate(): scaled = coupling * vector  13.2 us
    slice x14, local copies, waits for them, and re-layouts, with_halo(): lax.slice_in_dim(block, 0, width, axis=dim)  13 us
  transfers between devices with their start and end apart: 29, of which 15 were waited for; matrix products, arithmetic and copies ran while one was open for 4% of the time, Pallas kernels for 0%

profile of v1, /device:TPU:0, one launch (start us, length us, event | category | flops | bytes accessed | tf_op | source)
XLA Modules:
  0.0 358.9 jit_solution(3629934443591543465)
XLA Ops:
  5.1 5.5 %collective-permute-start.2 = (f32[80,2,256]{2,1,0:T(2,128)S(1)}, f32[80,2,256]{2,1,0:T(2,128)S(1)}, u32[]{:S(2)}, u32[]{:S(2)}) collective-permute-start(f32[80,2,256]{2,1,0:T(2,128)S(1)} %get-tuple-element.115), channel_id=1, source_target_pairs={{0,4},{4,8},{8,12},{1,5},{5,9},{9,13},{2,6},{6,10},{10,14},{3,7},{... | collective-permute-start | bytes 491528 | tf_op jit(solution)/shard_map/ppermute | solution.py:32
  16.4 4.5 %collective-permute-start.4 = (f32[80,12,2]{0,2,1:T(2,128)S(1)}, f32[80,12,2]{0,2,1:T(2,128)S(1)}, u32[]{:S(2)}, u32[]{:S(2)}) collective-permute-start(f32[80,12,2]{0,2,1:T(2,128)S(1)} %copy.16), channel_id=1, source_target_pairs={{0,1},{1,2},{2,3},{4,5},{5,6},{6,7},{8,9},{9,10},{10,11},{12,13},{... | collective-permute-start | bytes 23048 | tf_op jit(solution)/shard_map/ppermute | solution.py:32
  22.7 1.5 pad_maximum_fusion
  24.3 2.8 fusion.132
  28.6 5.2 %collective-permute-start.6 = (f32[80,2,256]{2,1,0:T(2,128)S(1)}, f32[80,2,256]{2,1,0:T(2,128)S(1)}, u32[]{:S(2)}, u32[]{:S(2)}) collective-permute-start(f32[80,2,256]{2,1,0:T(2,128)S(1)} %get-tuple-element.111), channel_id=1, source_target_pairs={{0,4},{4,8},{8,12},{1,5},{5,9},{9,13},{2,6},{6,10},{10,14},{3,7},{... | collective-permute-start | bytes 491528 | tf_op jit(solution)/shard_map/ppermute | solution.py:32
  33.8 1.3 collective-permute-done.5
  35.1 1.5 collective-permute-done.6
  37.9 1.3 copy.18
  40.7 4.8 %collective-permute-start.8 = (f32[80,12,2]{0,2,1:T(2,128)S(1)}, f32[80,12,2]{0,2,1:T(2,128)S(1)}, u32[]{:S(2)}, u32[]{:S(2)}) collective-permute-start(f32[80,12,2]{0,2,1:T(2,128)S(1)} %copy.20), channel_id=1, source_target_pairs={{0,1},{1,2},{2,3},{4,5},{5,6},{6,7},{8,9},{9,10},{10,11},{12,13},{... | collective-permute-start | bytes 23048 | tf_op jit(solution)/shard_map/ppermute | solution.py:32
  49.0 2.9 pad_maximum_fusion.1
  52.0 3.4 multiply_reduce_fusion.10
  55.4 13.0 %all-reduce.19 = (f32[]{:T(128)}, f32[]{:T(128)}) all-reduce(f32[]{:T(128)} %get-tuple-element.15, f32[]{:T(128)} %get-tuple-element.14), channel_id=1, replica_groups=mesh['group'=2,'gx'=4,'gy'=4] {'gy'}, use_global_device_ids=true, to_apply=%region_2.3 | all-reduce | flops 2 | bytes 16 | tf_op jit(solution)/shard_map/psum | solution.py:75
  68.3 13.9 %all-reduce.25 = (f32[]{:T(128)}, f32[]{:T(128)}) all-reduce(f32[]{:T(128)} %get-tuple-element.26, f32[]{:T(128)} %get-tuple-element.27), channel_id=1, replica_groups=mesh['group'=2,'gx'=4,'gy'=4] {'gx'}, use_global_device_ids=true, to_apply=%region_3.4 | all-reduce | flops 2 | bytes 16 | tf_op jit(solution)/shard_map/psum | solution.py:76
  83.6 1.5 fusion.131
  85.2 1.9 collective-permute-start.10
  88.5 1.5 collective-permute-done.10
  90.0 4.4 %collective-permute-done.9 = f32[80,2,256]{2,1,0:T(2,128)S(1)} collective-permute-done((f32[80,2,256]{2,1,0:T(2,128)S(1)}, f32[80,2,256]{2,1,0:T(2,128)S(1)}, u32[]{:S(2)}, u32[]{:S(2)}) %collective-permute-start.9) | collective-permute-done | bytes 163872 | tf_op jit(solution)/shard_map/ppermute | solution.py:35
  95.7 1.3 copy.22
  98.6 4.7 %collective-permute-start.12 = (f32[80,12,2]{0,2,1:T(2,128)S(1)}, f32[80,12,2]{0,2,1:T(2,128)S(1)}, u32[]{:S(2)}, u32[]{:S(2)}) collective-permute-start(f32[80,12,2]{0,2,1:T(2,128)S(1)} %copy.24), channel_id=1, source_target_pairs={{0,1},{1,2},{2,3},{4,5},{5,6},{6,7},{8,9},{9,10},{10,11},{12,13},{... | collective-permute-start | bytes 23048 | tf_op jit(solution)/shard_map/ppermute | solution.py:32
  106.0 2.7 pad_maximum_fusion.2
  108.7 3.4 multiply_reduce_fusion.8
  112.2 10.9 %all-reduce.18 = (f32[]{:T(128)}, f32[]{:T(128)}) all-reduce(f32[]{:T(128)} %get-tuple-element.11, f32[]{:T(128)} %get-tuple-element.10), channel_id=1, replica_groups=mesh['group'=2,'gx'=4,'gy'=4] {'gy'}, use_global_device_ids=true, to_apply=%region_8.9 | all-reduce | flops 2 | bytes 16 | tf_op jit(solution)/shard_map/psum | solution.py:75
  123.1 11.0 %all-reduce.24 = (f32[]{:T(128)}, f32[]{:T(128)}) all-reduce(f32[]{:T(128)} %get-tuple-element.24, f32[]{:T(128)} %get-tuple-element.25), channel_id=1, replica_groups=mesh['group'=2,'gx'=4,'gy'=4] {'gx'}, use_global_device_ids=true, to_apply=%region_9.10 | all-reduce | flops 2 | bytes 16 | tf_op jit(solution)/shard_map/psum | solution.py:76
  138.8 1.6 fusion.130
  141.9 4.6 %collective-permute-start.14 = (f32[80,2,256]{2,1,0:T(2,128)S(1)}, f32[80,2,256]{2,1,0:T(2,128)S(1)}, u32[]{:S(2)}, u32[]{:S(2)}) collective-permute-start(f32[80,2,256]{2,1,0:T(2,128)S(1)} %get-tuple-element.103), channel_id=1, source_target_pairs={{0,4},{4,8},{8,12},{1,5},{5,9},{9,13},{2,6},{6,10},{10,14},{3,7},{... | collective-permute-start | bytes 491528 | tf_op jit(solution)/shard_map/ppermute | solution.py:32
  146.4 1.3 collective-permute-done.13
  147.8 1.5 collective-permute-done.14
  150.7 1.3 copy.26
  153.3 1.3 copy.28
  154.7 4.5 %collective-permute-start.16 = (f32[80,12,2]{0,2,1:T(2,128)S(1)}, f32[80,12,2]{0,2,1:T(2,128)S(1)}, u32[]{:S(2)}, u32[]{:S(2)}) collective-permute-start(f32[80,12,2]{0,2,1:T(2,128)S(1)} %copy.28), channel_id=1, source_target_pairs={{0,1},{1,2},{2,3},{4,5},{5,6},{6,7},{8,9},{9,10},{10,11},{12,13},{... | collective-permute-start | bytes 23048 | tf_op jit(solution)/shard_map/ppermute | solution.py:32
  162.7 2.9 pad_maximum_fusion.3
  165.6 3.4 multiply_reduce_fusion.6
  168.9 10.4 %all-reduce.17 = (f32[]{:T(128)}, f32[]{:T(128)}) all-reduce(f32[]{:T(128)} %get-tuple-element.9, f32[]{:T(128)} %get-tuple-element.8), channel_id=1, replica_groups=mesh['group'=2,'gx'=4,'gy'=4] {'gy'}, use_global_device_ids=true, to_apply=%region_14.15 | all-reduce | flops 2 | bytes 16 | tf_op jit(solution)/shard_map/psum | solution.py:75
  179.3 11.6 %all-reduce.23 = (f32[]{:T(128)}, f32[]{:T(128)}) all-reduce(f32[]{:T(128)} %get-tuple-element.22, f32[]{:T(128)} %get-tuple-element.23), channel_id=1, replica_groups=mesh['group'=2,'gx'=4,'gy'=4] {'gx'}, use_global_device_ids=true, to_apply=%region_15.16 | all-reduce | flops 2 | bytes 16 | tf_op jit(solution)/shard_map/psum | solution.py:76
  194.6 2.7 fusion.129
  198.7 4.6 %collective-permute-start.18 = (f32[80,2,256]{2,1,0:T(2,128)S(1)}, f32[80,2,256]{2,1,0:T(2,128)S(1)}, u32[]{:S(2)}, u32[]{:S(2)}) collective-permute-start(f32[80,2,256]{2,1,0:T(2,128)S(1)} %get-tuple-element.99), channel_id=1, source_target_pairs={{0,4},{4,8},{8,12},{1,5},{5,9},{9,13},{2,6},{6,10},{10,14},{3,7},{... | collective-permute-start | bytes 491528 | tf_op jit(solution)/shard_map/ppermute | solution.py:32
  203.3 1.3 collective-permute-done.17
  204.6 1.5 collective-permute-done.18
  208.4 4.8 %collective-permute-start.20 = (f32[80,12,2]{0,2,1:T(2,128)S(1)}, f32[80,12,2]{0,2,1:T(2,128)S(1)}, u32[]{:S(2)}, u32[]{:S(2)}) collective-permute-start(f32[80,12,2]{0,2,1:T(2,128)S(1)} %copy.32), channel_id=1, source_target_pairs={{0,1},{1,2},{2,3},{4,5},{5,6},{6,7},{8,9},{9,10},{10,11},{12,13},{... | collective-permute-start | bytes 23048 | tf_op jit(solution)/shard_map/ppermute | solution.py:32
  215.1 1.5 pad_maximum_fusion.4
  216.6 3.4 multiply_reduce_fusion.4
  220.0 11.0 %all-reduce.16 = (f32[]{:T(128)}, f32[]{:T(128)}) all-reduce(f32[]{:T(128)} %get-tuple-element.7, f32[]{:T(128)} %get-tuple-element.6), channel_id=1, replica_groups=mesh['group'=2,'gx'=4,'gy'=4] {'gy'}, use_global_device_ids=true, to_apply=%region_20.21 | all-reduce | flops 2 | bytes 16 | tf_op jit(solution)/shard_map/psum | solution.py:75
  230.9 10.6 %all-reduce.22 = (f32[]{:T(128)}, f32[]{:T(128)}) all-reduce(f32[]{:T(128)} %get-tuple-element.20, f32[]{:T(128)} %get-tuple-element.21), channel_id=1, replica_groups=mesh['group'=2,'gx'=4,'gy'=4] {'gx'}, use_global_device_ids=true, to_apply=%region_21.22 | all-reduce | flops 2 | bytes 16 | tf_op jit(solution)/shard_map/psum | solution.py:76
  245.2 1.8 fusion.128
  248.4 4.6 %collective-permute-start.22 = (f32[80,2,256]{2,1,0:T(2,128)S(1)}, f32[80,2,256]{2,1,0:T(2,128)S(1)}, u32[]{:S(2)}, u32[]{:S(2)}) collective-permute-start(f32[80,2,256]{2,1,0:T(2,128)S(1)} %get-tuple-element.95), channel_id=1, source_target_pairs={{0,4},{4,8},{8,12},{1,5},{5,9},{9,13},{2,6},{6,10},{10,14},{3,7},{... | collective-permute-start | bytes 491528 | tf_op jit(solution)/shard_map/ppermute | solution.py:32
  253.0 1.3 collective-permute-done.21
  254.3 1.5 collective-permute-done.22
  257.1 1.3 copy.34
  260.0 4.5 %collective-permute-start.24 = (f32[80,12,2]{0,2,1:T(2,128)S(1)}, f32[80,12,2]{0,2,1:T(2,128)S(1)}, u32[]{:S(2)}, u32[]{:S(2)}) collective-permute-start(f32[80,12,2]{0,2,1:T(2,128)S(1)} %copy.36), channel_id=1, source_target_pairs={{0,1},{1,2},{2,3},{4,5},{5,6},{6,7},{8,9},{9,10},{10,11},{12,13},{... | collective-permute-start | bytes 23048 | tf_op jit(solution)/shard_map/ppermute | solution.py:32
  267.2 2.7 pad_maximum_fusion.5
  269.9 3.3 multiply_reduce_fusion.2
  273.3 11.2 %all-reduce.15 = (f32[]{:T(128)}, f32[]{:T(128)}) all-reduce(f32[]{:T(128)} %get-tuple-element.5, f32[]{:T(128)} %get-tuple-element.4), channel_id=1, replica_groups=mesh['group'=2,'gx'=4,'gy'=4] {'gy'}, use_global_device_ids=true, to_apply=%region_26.27 | all-reduce | flops 2 | bytes 16 | tf_op jit(solution)/shard_map/psum | solution.py:75
  284.4 11.5 %all-reduce.21 = (f32[]{:T(128)}, f32[]{:T(128)}) all-reduce(f32[]{:T(128)} %get-tuple-element.18, f32[]{:T(128)} %get-tuple-element.19), channel_id=1, replica_groups=mesh['group'=2,'gx'=4,'gy'=4] {'gx'}, use_global_device_ids=true, to_apply=%region_27.28 | all-reduce | flops 2 | bytes 16 | tf_op jit(solution)/shard_map/psum | solution.py:76
  299.8 2.7 fusion.127
  303.9 4.6 %collective-permute-start.26 = (f32[80,2,256]{2,1,0:T(2,128)S(1)}, f32[80,2,256]{2,1,0:T(2,128)S(1)}, u32[]{:S(2)}, u32[]{:S(2)}) collective-permute-start(f32[80,2,256]{2,1,0:T(2,128)S(1)} %get-tuple-element.91), channel_id=1, source_target_pairs={{0,4},{4,8},{8,12},{1,5},{5,9},{9,13},{2,6},{6,10},{10,14},{3,7},{... | collective-permute-start | bytes 491528 | tf_op jit(solution)/shard_map/ppermute | solution.py:32
  308.5 1.5 collective-permute-done.25
  310.0 1.3 collective-permute-done.26
  312.6 1.3 copy.38
  315.5 4.8 %collective-permute-start.28 = (f32[80,12,2]{0,2,1:T(2,128)S(1)}, f32[80,12,2]{0,2,1:T(2,128)S(1)}, u32[]{:S(2)}, u32[]{:S(2)}) collective-permute-start(f32[80,12,2]{0,2,1:T(2,128)S(1)} %copy.40), channel_id=1, source_target_pairs={{0,1},{1,2},{2,3},{4,5},{5,6},{6,7},{8,9},{9,10},{10,11},{12,13},{... | collective-permute-start | bytes 23048 | tf_op jit(solution)/shard_map/ppermute | solution.py:32
  322.9 2.7 pad_maximum_fusion.6
  325.7 3.4 multiply_reduce_fusion
  329.1 10.9 %all-reduce.14 = (f32[]{:T(128)}, f32[]{:T(128)}) all-reduce(f32[]{:T(128)} %get-tuple-element.13, f32[]{:T(128)} %get-tuple-element.12), channel_id=1, replica_groups=mesh['group'=2,'gx'=4,'gy'=4] {'gy'}, use_global_device_ids=true, to_apply=%region_32.33 | all-reduce | flops 2 | bytes 16 | tf_op jit(solution)/shard_map/psum | solution.py:75
  340.1 10.7 %all-reduce.20 = (f32[]{:T(128)}, f32[]{:T(128)}) all-reduce(f32[]{:T(128)} %get-tuple-element.16, f32[]{:T(128)} %get-tuple-element.17), channel_id=1, replica_groups=mesh['group'=2,'gx'=4,'gy'=4] {'gx'}, use_global_device_ids=true, to_apply=%region_33.34 | all-reduce | flops 2 | bytes 16 | tf_op jit(solution)/shard_map/psum | solution.py:76
  354.8 3.2 add_bitcast_fusion
  (146 shorter events, 54.7 us)
Async XLA Ops:
  3.8 9.1 %collective-permute-start.1 = (f32[80,2,256]{2,1,0:T(2,128)S(1)}, f32[80,2,256]{2,1,0:T(2,128)S(1)}, u32[]{:S(2)}, u32[]{:S(2)}) collective-permute-start(f32[80,2,256]{2,1,0:T(2,128)S(1)} %get-tuple-element.116), channel_id=1, source_target_pairs={{4,0},{8,4},{12,8},{5,1},{9,5},{13,9},{6,2},{10,6},{14,10},{7,3},{... | collective-permute-start | bytes 491528 | tf_op jit(solution)/shard_map/ppermute | solution.py:35
  5.1 8.9 %collective-permute-start.2 = (f32[80,2,256]{2,1,0:T(2,128)S(1)}, f32[80,2,256]{2,1,0:T(2,128)S(1)}, u32[]{:S(2)}, u32[]{:S(2)}) collective-permute-start(f32[80,2,256]{2,1,0:T(2,128)S(1)} %get-tuple-element.115), channel_id=1, source_target_pairs={{0,4},{4,8},{8,12},{1,5},{5,9},{9,13},{2,6},{6,10},{10,14},{3,7},{... | collective-permute-start | bytes 491528 | tf_op jit(solution)/shard_map/ppermute | solution.py:32
  10.7 10.3 %collective-permute-start = (f32[2,8,256]{2,1,0:T(8,128)S(1)}, f32[2,8,256]{2,1,0:T(8,128)S(1)}, u32[]{:S(2)}, u32[]{:S(2)}) collective-permute-start(f32[2,8,256]{2,1,0:T(8,128)S(1)} %pad_maximum_fusion.28), channel_id=1, source_target_pairs={{0,16},{16,0},{1,17},{17,1},{2,18},{18,2},{3,19},{19,3},{4,20},{20... | collective-permute-start | bytes 49160 | tf_op jit(solution)/shard_map/ppermute | solution.py:41
  14.8 6.1 %collective-permute-start.3 = (f32[80,12,2]{0,2,1:T(2,128)S(1)}, f32[80,12,2]{0,2,1:T(2,128)S(1)}, u32[]{:S(2)}, u32[]{:S(2)}) collective-permute-start(f32[80,12,2]{0,2,1:T(2,128)S(1)} %copy.14), channel_id=1, source_target_pairs={{1,0},{2,1},{3,2},{5,4},{6,5},{7,6},{9,8},{10,9},{11,10},{13,12},{... | collective-permute-start | bytes 23048 | tf_op jit(solution)/shard_map/ppermute | solution.py:35
  16.4 5.9 %collective-permute-start.4 = (f32[80,12,2]{0,2,1:T(2,128)S(1)}, f32[80,12,2]{0,2,1:T(2,128)S(1)}, u32[]{:S(2)}, u32[]{:S(2)}) collective-permute-start(f32[80,12,2]{0,2,1:T(2,128)S(1)} %copy.16), channel_id=1, source_target_pairs={{0,1},{1,2},{2,3},{4,5},{5,6},{6,7},{8,9},{9,10},{10,11},{12,13},{... | collective-permute-start | bytes 23048 | tf_op jit(solution)/shard_map/ppermute | solution.py:32
  22.7 1.5 copy-start
  22.7 1.5 copy-start.1
  22.7 1.5 copy-start.13
  22.7 1.6 copy-start.14
  22.7 1.6 copy-start.27
  27.3 7.8 %collective-permute-start.5 = (f32[80,2,256]{2,1,0:T(2,128)S(1)}, f32[80,2,256]{2,1,0:T(2,128)S(1)}, u32[]{:S(2)}, u32[]{:S(2)}) collective-permute-start(f32[80,2,256]{2,1,0:T(2,128)S(1)} %get-tuple-element.112), channel_id=1, source_target_pairs={{4,0},{8,4},{12,8},{5,1},{9,5},{13,9},{6,2},{10,6},{14,10},{7,3},{... | collective-permute-start | bytes 491528 | tf_op jit(solution)/shard_map/ppermute | solution.py:35
  28.6 8.0 %collective-permute-start.6 = (f32[80,2,256]{2,1,0:T(2,128)S(1)}, f32[80,2,256]{2,1,0:T(2,128)S(1)}, u32[]{:S(2)}, u32[]{:S(2)}) collective-permute-start(f32[80,2,256]{2,1,0:T(2,128)S(1)} %get-tuple-element.111), channel_id=1, source_target_pairs={{0,4},{4,8},{8,12},{1,5},{5,9},{9,13},{2,6},{6,10},{10,14},{3,7},{... | collective-permute-start | bytes 491528 | tf_op jit(solution)/shard_map/ppermute | solution.py:32
  39.2 7.5 %collective-permute-start.7 = (f32[80,12,2]{0,2,1:T(2,128)S(1)}, f32[80,12,2]{0,2,1:T(2,128)S(1)}, u32[]{:S(2)}, u32[]{:S(2)}) collective-permute-start(f32[80,12,2]{0,2,1:T(2,128)S(1)} %copy.18), channel_id=1, source_target_pairs={{1,0},{2,1},{3,2},{5,4},{6,5},{7,6},{9,8},{10,9},{11,10},{13,12},{... | collective-permute-start | bytes 23048 | tf_op jit(solution)/shard_map/ppermute | solution.py:35
  40.7 7.1 %collective-permute-start.8 = (f32[80,12,2]{0,2,1:T(2,128)S(1)}, f32[80,12,2]{0,2,1:T(2,128)S(1)}, u32[]{:S(2)}, u32[]{:S(2)}) collective-permute-start(f32[80,12,2]{0,2,1:T(2,128)S(1)} %copy.20), channel_id=1, source_target_pairs={{0,1},{1,2},{2,3},{4,5},{5,6},{6,7},{8,9},{9,10},{10,11},{12,13},{... | collective-permute-start | bytes 23048 | tf_op jit(solution)/shard_map/ppermute | solution.py:32
  49.0 2.9 copy-start.7
  49.0 2.9 copy-start.17
  49.0 2.9 copy-start.18
  85.1 23.6 %copy-start.6 = (f32[80,8,256]{2,1,0:T(8,128)}, f32[80,8,256]{2,1,0:T(8,128)S(1)}, u32[]{:S(2)}) copy-start(f32[80,8,256]{2,1,0:T(8,128)S(1)} %get-tuple-element.56) | copy-start | bytes 1966084
  85.2 4.7 %collective-permute-start.10 = (f32[80,2,256]{2,1,0:T(2,128)S(1)}, f32[80,2,256]{2,1,0:T(2,128)S(1)}, u32[]{:S(2)}, u32[]{:S(2)}) collective-permute-start(f32[80,2,256]{2,1,0:T(2,128)S(1)} %get-tuple-element.107), channel_id=1, source_target_pairs={{0,4},{4,8},{8,12},{1,5},{5,9},{9,13},{2,6},{6,10},{10,14},{3,7},{... | collective-permute-start | bytes 491528 | tf_op jit(solution)/shard_map/ppermute | solution.py:32
  87.2 7.2 %collective-permute-start.9 = (f32[80,2,256]{2,1,0:T(2,128)S(1)}, f32[80,2,256]{2,1,0:T(2,128)S(1)}, u32[]{:S(2)}, u32[]{:S(2)}) collective-permute-start(f32[80,2,256]{2,1,0:T(2,128)S(1)} %get-tuple-element.108), channel_id=1, source_target_pairs={{4,0},{8,4},{12,8},{5,1},{9,5},{13,9},{6,2},{10,6},{14,10},{7,3},{... | collective-permute-start | bytes 491528 | tf_op jit(solution)/shard_map/ppermute | solution.py:35
  97.0 7.4 %collective-permute-start.11 = (f32[80,12,2]{0,2,1:T(2,128)S(1)}, f32[80,12,2]{0,2,1:T(2,128)S(1)}, u32[]{:S(2)}, u32[]{:S(2)}) collective-permute-start(f32[80,12,2]{0,2,1:T(2,128)S(1)} %copy.22), channel_id=1, source_target_pairs={{1,0},{2,1},{3,2},{5,4},{6,5},{7,6},{9,8},{10,9},{11,10},{13,12},{... | collective-permute-start | bytes 23048 | tf_op jit(solution)/shard_map/ppermute | solution.py:35
  98.6 6.3 %collective-permute-start.12 = (f32[80,12,2]{0,2,1:T(2,128)S(1)}, f32[80,12,2]{0,2,1:T(2,128)S(1)}, u32[]{:S(2)}, u32[]{:S(2)}) collective-permute-start(f32[80,12,2]{0,2,1:T(2,128)S(1)} %copy.24), channel_id=1, source_target_pairs={{0,1},{1,2},{2,3},{4,5},{5,6},{6,7},{8,9},{9,10},{10,11},{12,13},{... | collective-permute-start | bytes 23048 | tf_op jit(solution)/shard_map/ppermute | solution.py:32
  106.0 2.7 copy-start.19
  106.0 2.7 copy-start.20
  108.7 30.1 %copy-start.2 = (f32[80,8,256]{2,1,0:T(8,128)S(1)}, f32[80,8,256]{2,1,0:T(8,128)}, u32[]{:S(2)}) copy-start(f32[80,8,256]{2,1,0:T(8,128)} %get-tuple-element.57) | copy-start | bytes 1966084
  140.4 54.1 %copy-start.3 = (f32[80,8,256]{2,1,0:T(8,128)}, f32[80,8,256]{2,1,0:T(8,128)S(1)}, u32[]{:S(2)}) copy-start(f32[80,8,256]{2,1,0:T(8,128)S(1)} %get-tuple-element.53) | copy-start | bytes 1966084
  140.6 7.2 %collective-permute-start.13 = (f32[80,2,256]{2,1,0:T(2,128)S(1)}, f32[80,2,256]{2,1,0:T(2,128)S(1)}, u32[]{:S(2)}, u32[]{:S(2)}) collective-permute-start(f32[80,2,256]{2,1,0:T(2,128)S(1)} %get-tuple-element.104), channel_id=1, source_target_pairs={{4,0},{8,4},{12,8},{5,1},{9,5},{13,9},{6,2},{10,6},{14,10},{7,3},{... | collective-permute-start | bytes 491528 | tf_op jit(solution)/shard_map/ppermute | solution.py:35
  141.9 7.4 %collective-permute-start.14 = (f32[80,2,256]{2,1,0:T(2,128)S(1)}, f32[80,2,256]{2,1,0:T(2,128)S(1)}, u32[]{:S(2)}, u32[]{:S(2)}) collective-permute-start(f32[80,2,256]{2,1,0:T(2,128)S(1)} %get-tuple-element.103), channel_id=1, source_target_pairs={{0,4},{4,8},{8,12},{1,5},{5,9},{9,13},{2,6},{6,10},{10,14},{3,7},{... | collective-permute-start | bytes 491528 | tf_op jit(solution)/shard_map/ppermute | solution.py:32
  152.1 8.3 %collective-permute-start.15 = (f32[80,12,2]{0,2,1:T(2,128)S(1)}, f32[80,12,2]{0,2,1:T(2,128)S(1)}, u32[]{:S(2)}, u32[]{:S(2)}) collective-permute-start(f32[80,12,2]{0,2,1:T(2,128)S(1)} %copy.26), channel_id=1, source_target_pairs={{1,0},{2,1},{3,2},{5,4},{6,5},{7,6},{9,8},{10,9},{11,10},{13,12},{... | collective-permute-start | bytes 23048 | tf_op jit(solution)/shard_map/ppermute | solution.py:35
  154.7 6.9 %collective-permute-start.16 = (f32[80,12,2]{0,2,1:T(2,128)S(1)}, f32[80,12,2]{0,2,1:T(2,128)S(1)}, u32[]{:S(2)}, u32[]{:S(2)}) collective-permute-start(f32[80,12,2]{0,2,1:T(2,128)S(1)} %copy.28), channel_id=1, source_target_pairs={{0,1},{1,2},{2,3},{4,5},{5,6},{6,7},{8,9},{9,10},{10,11},{12,13},{... | collective-permute-start | bytes 23048 | tf_op jit(solution)/shard_map/ppermute | solution.py:32
  162.7 2.9 copy-start.21
  162.7 2.9 copy-start.22
  197.4 7.2 %collective-permute-start.17 = (f32[80,2,256]{2,1,0:T(2,128)S(1)}, f32[80,2,256]{2,1,0:T(2,128)S(1)}, u32[]{:S(2)}, u32[]{:S(2)}) collective-permute-start(f32[80,2,256]{2,1,0:T(2,128)S(1)} %get-tuple-element.100), channel_id=1, source_target_pairs={{4,0},{8,4},{12,8},{5,1},{9,5},{13,9},{6,2},{10,6},{14,10},{7,3},{... | collective-permute-start | bytes 491528 | tf_op jit(solution)/shard_map/ppermute | solution.py:35
  198.7 7.4 %collective-permute-start.18 = (f32[80,2,256]{2,1,0:T(2,128)S(1)}, f32[80,2,256]{2,1,0:T(2,128)S(1)}, u32[]{:S(2)}, u32[]{:S(2)}) collective-permute-start(f32[80,2,256]{2,1,0:T(2,128)S(1)} %get-tuple-element.99), channel_id=1, source_target_pairs={{0,4},{4,8},{8,12},{1,5},{5,9},{9,13},{2,6},{6,10},{10,14},{3,7},{... | collective-permute-start | bytes 491528 | tf_op jit(solution)/shard_map/ppermute | solution.py:32
  206.8 7.5 %collective-permute-start.19 = (f32[80,12,2]{0,2,1:T(2,128)S(1)}, f32[80,12,2]{0,2,1:T(2,128)S(1)}, u32[]{:S(2)}, u32[]{:S(2)}) collective-permute-start(f32[80,12,2]{0,2,1:T(2,128)S(1)} %copy.30), channel_id=1, source_target_pairs={{1,0},{2,1},{3,2},{5,4},{6,5},{7,6},{9,8},{10,9},{11,10},{13,12},{... | collective-permute-start | bytes 23048 | tf_op jit(solution)/shard_map/ppermute | solution.py:35
  208.4 6.3 %collective-permute-start.20 = (f32[80,12,2]{0,2,1:T(2,128)S(1)}, f32[80,12,2]{0,2,1:T(2,128)S(1)}, u32[]{:S(2)}, u32[]{:S(2)}) collective-permute-start(f32[80,12,2]{0,2,1:T(2,128)S(1)} %copy.32), channel_id=1, source_target_pairs={{0,1},{1,2},{2,3},{4,5},{5,6},{6,7},{8,9},{9,10},{10,11},{12,13},{... | collective-permute-start | bytes 23048 | tf_op jit(solution)/shard_map/ppermute | solution.py:32
  215.1 1.5 copy-start.5
  215.1 1.5 copy-start.25
  215.1 1.5 copy-start.26
  247.1 7.2 %collective-permute-start.21 = (f32[80,2,256]{2,1,0:T(2,128)S(1)}, f32[80,2,256]{2,1,0:T(2,128)S(1)}, u32[]{:S(2)}, u32[]{:S(2)}) collective-permute-start(f32[80,2,256]{2,1,0:T(2,128)S(1)} %get-tuple-element.96), channel_id=1, source_target_pairs={{4,0},{8,4},{12,8},{5,1},{9,5},{13,9},{6,2},{10,6},{14,10},{7,3},{... | collective-permute-start | bytes 491528 | tf_op jit(solution)/shard_map/ppermute | solution.py:35
  248.4 7.4 %collective-permute-start.22 = (f32[80,2,256]{2,1,0:T(2,128)S(1)}, f32[80,2,256]{2,1,0:T(2,128)S(1)}, u32[]{:S(2)}, u32[]{:S(2)}) collective-permute-start(f32[80,2,256]{2,1,0:T(2,128)S(1)} %get-tuple-element.95), channel_id=1, source_target_pairs={{0,4},{4,8},{8,12},{1,5},{5,9},{9,13},{2,6},{6,10},{10,14},{3,7},{... | collective-permute-start | bytes 491528 | tf_op jit(solution)/shard_map/ppermute | solution.py:32
  258.4 7.2 %collective-permute-start.23 = (f32[80,12,2]{0,2,1:T(2,128)S(1)}, f32[80,12,2]{0,2,1:T(2,128)S(1)}, u32[]{:S(2)}, u32[]{:S(2)}) collective-permute-start(f32[80,12,2]{0,2,1:T(2,128)S(1)} %copy.34), channel_id=1, source_target_pairs={{1,0},{2,1},{3,2},{5,4},{6,5},{7,6},{9,8},{10,9},{11,10},{13,12},{... | collective-permute-start | bytes 23048 | tf_op jit(solution)/shard_map/ppermute | solution.py:35
  260.0 6.1 %collective-permute-start.24 = (f32[80,12,2]{0,2,1:T(2,128)S(1)}, f32[80,12,2]{0,2,1:T(2,128)S(1)}, u32[]{:S(2)}, u32[]{:S(2)}) collective-permute-start(f32[80,12,2]{0,2,1:T(2,128)S(1)} %copy.36), channel_id=1, source_target_pairs={{0,1},{1,2},{2,3},{4,5},{5,6},{6,7},{8,9},{9,10},{10,11},{12,13},{... | collective-permute-start | bytes 23048 | tf_op jit(solution)/shard_map/ppermute | solution.py:32
  267.2 2.7 copy-start.23
  267.2 2.7 copy-start.24
  269.9 29.9 %copy-start.8 = (f32[80,8,256]{2,1,0:T(8,128)S(1)}, f32[80,8,256]{2,1,0:T(8,128)}, u32[]{:S(2)}) copy-start(f32[80,8,256]{2,1,0:T(8,128)} %get-tuple-element.47) | copy-start | bytes 1966084
  302.6 7.3 %collective-permute-start.25 = (f32[80,2,256]{2,1,0:T(2,128)S(1)}, f32[80,2,256]{2,1,0:T(2,128)S(1)}, u32[]{:S(2)}, u32[]{:S(2)}) collective-permute-start(f32[80,2,256]{2,1,0:T(2,128)S(1)} %get-tuple-element.92), channel_id=1, source_target_pairs={{4,0},{8,4},{12,8},{5,1},{9,5},{13,9},{6,2},{10,6},{14,10},{7,3},{... | collective-permute-start | bytes 491528 | tf_op jit(solution)/shard_map/ppermute | solution.py:35
  303.9 7.4 %collective-permute-start.26 = (f32[80,2,256]{2,1,0:T(2,128)S(1)}, f32[80,2,256]{2,1,0:T(2,128)S(1)}, u32[]{:S(2)}, u32[]{:S(2)}) collective-permute-start(f32[80,2,256]{2,1,0:T(2,128)S(1)} %get-tuple-element.91), channel_id=1, source_target_pairs={{0,4},{4,8},{8,12},{1,5},{5,9},{9,13},{2,6},{6,10},{10,14},{3,7},{... | collective-permute-start | bytes 491528 | tf_op jit(solution)/shard_map/ppermute | solution.py:32
  313.9 7.5 %collective-permute-start.27 = (f32[80,12,2]{0,2,1:T(2,128)S(1)}, f32[80,12,2]{0,2,1:T(2,128)S(1)}, u32[]{:S(2)}, u32[]{:S(2)}) collective-permute-start(f32[80,12,2]{0,2,1:T(2,128)S(1)} %copy.38), channel_id=1, source_target_pairs={{1,0},{2,1},{3,2},{5,4},{6,5},{7,6},{9,8},{10,9},{11,10},{13,12},{... | collective-permute-start | bytes 23048 | tf_op jit(solution)/shard_map/ppermute | solution.py:35
  315.5 6.3 %collective-permute-start.28 = (f32[80,12,2]{0,2,1:T(2,128)S(1)}, f32[80,12,2]{0,2,1:T(2,128)S(1)}, u32[]{:S(2)}, u32[]{:S(2)}) collective-permute-start(f32[80,12,2]{0,2,1:T(2,128)S(1)} %copy.40), channel_id=1, source_target_pairs={{0,1},{1,2},{2,3},{4,5},{5,6},{6,7},{8,9},{9,10},{10,11},{12,13},{... | collective-permute-start | bytes 23048 | tf_op jit(solution)/shard_map/ppermute | solution.py:32
  322.9 2.7 copy-start.9
  322.9 2.7 copy-start.11
  322.9 2.7 copy-start.15
  322.9 2.8 copy-start.16
  325.7 29.1 %copy-start.4 = (f32[80,8,256]{2,1,0:T(8,128)S(1)}, f32[80,8,256]{2,1,0:T(8,128)}, u32[]{:S(2)}) copy-start(f32[80,8,256]{2,1,0:T(8,128)} %copy-done.3) | copy-start | bytes 1966084
  354.8 3.2 copy-start.10
  354.8 3.2 copy-start.12
